TPU v7x, 32 devices: a whole 2x2x4 slice. The times are simulated.
32 devices in a mesh: gx: 4 (over y, core), gy: 4 (over z), gz: 2 (over x).
Axes of the slice: x: 2, y: 2, z: 4, core: 2. Of those that a mesh axis runs over, the one named last changes fastest.
Arguments:
- fractions: float32 [3, 4, 8, 4, 128], P(None, 'gx', 'gy', 'gz'), may hold values from 0 to 1
- polarizability: float32 [4, 8, 4, 128], P('gx', 'gy', 'gz'), may hold values from 0.5 to 2
- occupancy: int32 [4, 8, 4, 128], P('gx', 'gy', 'gz'), may hold values 0 or 1
- pair_mask: int32 [4, 8, 4, 27], P('gx', 'gy', 'gz'), may hold values from 0 to 1, as said below
- perm_field: float32 [6, 4, 8, 4, 128], P(None, 'gx', 'gy', 'gz'), may hold values from -6 to 6
- history: float32 [6, 6, 4, 8, 4, 128], P(None, None, 'gx', 'gy', 'gz'), may hold values from -12 to 12
Outputs:
- induced: float32 [6, 4, 8, 4, 128], P(None, 'gx', 'gy', 'gz')
- change: float32 [], replicated
Inputs may be any that keep to these rules, and one draw needn't show every extreme that they name: pair_mask[t, k] equals pair_mask at tile t + offset(k) for the opposite offset 26 - k (periodic); pair_mask[t, 13] (the tile itself) is 1.
All inputs are finite; a program needn't handle non-finite values. No bound on the sum of `occupancy` on one device may be relied on, other than what follows from the above.
Results may differ from a plain program's by a relative error of at most 0.0003.
Values sent between devices are 32-bit elements; how exact they have to be, the bound alone decides.
A program may use at most 64 MiB of HBM per device.

v0:
```python
import jax
import jax.numpy as jnp
from jax import lax
from jax.sharding import PartitionSpec as P

CELL_EDGE = 10.0
SOFTENING = 0.3
THOLE_DAMP = 0.39
RELAXATION = 0.7


def with_halo(cells, sides, width):
    for axis, dim in sides:
        count = lax.axis_size(axis)
        head = lax.slice_in_dim(cells, 0, width, axis=dim)
        tail = lax.slice_in_dim(cells, cells.shape[dim] - width, cells.shape[dim], axis=dim)
        cells = jnp.concatenate(
            [
                lax.ppermute(tail, axis, [(i, (i + 1) % count) for i in range(count)]),
                cells,
                lax.ppermute(head, axis, [((i + 1) % count, i) for i in range(count)]),
            ],
            axis=dim,
        )
    return cells


def pair_field(target, source, moment, offset_vec, itself, allowed):
    displace = [
        (offset_vec[axis_num] + source[axis_num][:, None, :] - target[axis_num][:, :, None])
        * CELL_EDGE
        for axis_num in range(3)
    ]
    dist_sq = (
        displace[0] * displace[0]
        + displace[1] * displace[1]
        + displace[2] * displace[2]
        + SOFTENING
    )
    inv_cube = lax.rsqrt(dist_sq) / dist_sq
    thole_arg = (
        dist_sq * jnp.sqrt(dist_sq) * lax.rsqrt(target[3][:, :, None] * source[3][:, None, :])
    )
    damping = jnp.exp(-THOLE_DAMP * thole_arg)
    lambda_three = 1.0 - damping
    lambda_five = 1.0 - (1.0 + THOLE_DAMP * thole_arg) * damping
    slots = target.shape[-1]
    self_pair = jnp.logical_and(itself, jnp.eye(slots, dtype=bool))
    weight = jnp.where(self_pair, 0.0, allowed[:, None, None])
    radial = 3.0 * lambda_five * inv_cube / dist_sq * weight
    direct = lambda_three * inv_cube * weight
    fields = []
    for which_set in range(moment.shape[0] // 3):
        parts = [moment[3 * which_set + axis_num][:, None, :] for axis_num in range(3)]
        project = displace[0] * parts[0] + displace[1] * parts[1] + displace[2] * parts[2]
        for axis_num in range(3):
            fields.append(
                jnp.sum(radial * project * displace[axis_num] - direct * parts[axis_num], axis=-1)
            )
    return jnp.stack(fields)


def slab_field(geometry_pad, moment_pad, allowed_slab, slab_index):
    width_y = geometry_pad.shape[2] - 2
    width_z = geometry_pad.shape[3] - 2
    slots = geometry_pad.shape[4]
    rows = moment_pad.shape[0]
    zero = jnp.zeros((), jnp.int32)
    one = jnp.ones((), jnp.int32)
    first_x = (jnp.asarray(slab_index) + 1).astype(jnp.int32)
    target = lax.dynamic_slice(
        geometry_pad, (zero, first_x, one, one, zero), (4, 1, width_y, width_z, slots)
    ).reshape(4, width_y * width_z, slots)

    def offset_step(offset, summed):
        offset = jnp.asarray(offset).astype(jnp.int32)
        along_x = offset // 9 - 1
        along_y = offset // 3 % 3 - 1
        along_z = offset % 3 - 1
        starts = (zero, first_x + along_x, one + along_y, one + along_z, zero)
        source = lax.dynamic_slice(geometry_pad, starts, (4, 1, width_y, width_z, slots)).reshape(
            4, width_y * width_z, slots
        )
        moment = lax.dynamic_slice(moment_pad, starts, (rows, 1, width_y, width_z, slots)).reshape(
            rows, width_y * width_z, slots
        )
        allowed = (
            lax.dynamic_index_in_dim(allowed_slab, offset, 2, keepdims=False)
            .reshape(-1)
            .astype(jnp.float32)
        )
        offset_vec = jnp.stack([along_x, along_y, along_z]).astype(jnp.float32)
        return summed + pair_field(target, source, moment, offset_vec, offset == 13, allowed)

    summed = lax.fori_loop(
        0, 27, offset_step, jnp.zeros((rows, width_y * width_z, slots), jnp.float32)
    )
    return summed.reshape(rows, width_y, width_z, slots)


def device_field(geometry_pad, moment_pad, pair_mask):
    slabs = [slab_field(geometry_pad, moment_pad, pair_mask[0], 0)]
    return jnp.stack(slabs, 1)


def share_dipoles(dipoles):
    return with_halo(dipoles, (("gx", 1), ("gy", 2), ("gz", 3)), 1)


def global_gram(local_gram):
    return lax.psum(local_gram, ("gx", "gy", "gz"))


def fit_coefficients(gram_matrix):
    past_count = gram_matrix.shape[0] - 1
    gram_past = gram_matrix[:past_count, :past_count]
    gram_next = gram_matrix[:past_count, past_count]
    ridge_term = 0.001 * jnp.trace(gram_past) / past_count + 1.0
    factor = jnp.linalg.cholesky(gram_past + ridge_term * jnp.eye(past_count, dtype=jnp.float32))
    return jax.scipy.linalg.cho_solve((factor, True), gram_next)


def on_device(fractions, polarizability, occupancy, pair_mask, perm_field, history):
    filled = occupancy.astype(jnp.float32)
    geometry = jnp.concatenate([fractions, polarizability[None]], 0)
    masked = history * filled
    past_sets = masked.shape[0]
    flat_hist = masked.reshape(past_sets, -1)
    local_gram = jnp.dot(flat_hist, flat_hist.T, precision=lax.Precision.HIGHEST)
    scaled = RELAXATION * filled * polarizability
    later = masked[1:]
    coeffs = fit_coefficients(global_gram(local_gram))
    geometry_pad = with_halo(geometry, (("gx", 1), ("gy", 2), ("gz", 3)), 1)
    predicted = jnp.tensordot(coeffs, later, axes=1, precision=lax.Precision.HIGHEST)
    field_one = device_field(geometry_pad, share_dipoles(predicted), pair_mask)
    dipole_one = (1.0 - RELAXATION) * predicted + scaled * (perm_field + field_one)
    field_two = device_field(geometry_pad, share_dipoles(dipole_one), pair_mask)
    induced = (1.0 - RELAXATION) * dipole_one + scaled * (perm_field + field_two)
    update = induced - dipole_one
    totals = lax.psum((jnp.sum(update * update), jnp.sum(induced * induced)), ("gx", "gy", "gz"))
    change = jnp.sqrt(totals[0] / (totals[1] + 1.0))
    return (induced, change)


def solution(mesh):
    in_specs = (
        P(None, "gx", "gy", "gz", None),
        P("gx", "gy", "gz", None),
        P("gx", "gy", "gz", None),
        P("gx", "gy", "gz", None),
        P(None, "gx", "gy", "gz", None),
        P(None, None, "gx", "gy", "gz", None),
    )
    out_specs = (P(None, "gx", "gy", "gz", None), P())
    return jax.shard_map(
        on_device, mesh=mesh, in_specs=in_specs, out_specs=out_specs, check_vma=False
    )
```

profile of v0, /device:TPU:0, one launch (start us, length us, event | category | flops | bytes accessed | tf_op | source)
XLA Modules:
  0.0 395.9 jit_solution(7175893039068339655)
XLA Ops:
  3.1 42.0 %psum.21 = f32[6,6]{0,1:T(8,128)S(1)} all-reduce(f32[6,6]{0,1:T(8,128)S(1)} %convolution_bitcast_fusion), channel_id=1, replica_groups=mesh['gx'=4,'gy'=4,'gz'=2] {'gx','gy','gz'}, use_global_device_ids=true, to_apply=%region_0.0 | all-reduce | flops 36 | bytes 288 | tf_op jit(solution)/shard_map/psum | solution.py:111
  56.1 2.3 collective-permute-start.3
  58.6 3.8 collective-permute-start.9
  62.4 2.3 collective-permute-start.4
  65.0 2.0 collective-permute-start.10
  71.1 134.4 %while.38 = (s32[]{:T(128)}, f32[6,4,128]{2,1,0:T(4,128)S(1)}, f32[4,3,4,4,128]{4,3,2,1,0:T(4,128)S(1)}, f32[4,4,128]{2,1,0:T(4,128)S(1)}, s32[2,2,27]{1,0,2:T(2...) while((s32[]{:T(128)}, f32[6,4,128]{2,1,0:T(4,128)S(1)}, ...), condition=%wide.region_11.12_spmd.clone, body=%wide.region_4.11_spmd.clone.sunk | while | flops 6200888 | bytes 287493 | solution.py:95
  72.0 1.9 dynamic-slice_add_fusion.4
  77.0 1.9 dynamic-slice_add_fusion.4
  81.9 1.9 dynamic-slice_add_fusion.4
  86.9 1.9 dynamic-slice_add_fusion.4
  91.9 1.9 dynamic-slice_add_fusion.4
  96.9 1.9 dynamic-slice_add_fusion.4
  101.8 1.9 dynamic-slice_add_fusion.4
  106.8 1.9 dynamic-slice_add_fusion.4
  111.8 1.9 dynamic-slice_add_fusion.4
  116.8 1.9 dynamic-slice_add_fusion.4
  121.8 1.9 dynamic-slice_add_fusion.4
  126.7 1.9 dynamic-slice_add_fusion.4
  131.7 1.9 dynamic-slice_add_fusion.4
  136.7 1.9 dynamic-slice_add_fusion.4
  141.7 1.9 dynamic-slice_add_fusion.4
  146.6 1.9 dynamic-slice_add_fusion.4
  151.6 1.9 dynamic-slice_add_fusion.4
  156.6 1.9 dynamic-slice_add_fusion.4
  161.6 1.9 dynamic-slice_add_fusion.4
  166.6 1.9 dynamic-slice_add_fusion.4
  171.5 1.9 dynamic-slice_add_fusion.4
  176.5 1.9 dynamic-slice_add_fusion.4
  181.5 1.9 dynamic-slice_add_fusion.4
  186.5 1.9 dynamic-slice_add_fusion.4
  191.4 1.9 dynamic-slice_add_fusion.4
  196.4 1.9 dynamic-slice_add_fusion.4
  201.4 1.9 dynamic-slice_add_fusion.4
  208.8 3.8 collective-permute-start.15
  216.6 2.0 collective-permute-done.16
  219.1 133.6 %while.39 = (s32[]{:T(128)}, f32[6,4,128]{2,1,0:T(4,128)S(1)}, f32[4,3,4,4,128]{4,3,2,1,0:T(4,128)S(1)}, f32[4,4,128]{2,1,0:T(4,128)S(1)}, s32[2,2,27]{1,0,2:T(2...) while((s32[]{:T(128)}, f32[6,4,128]{2,1,0:T(4,128)S(1)}, ...), condition=%wide.region_19.20_spmd.clone, body=%wide.region_12.19_spmd.clone.sunk | while | flops 6200890 | bytes 262953 | solution.py:95
  219.9 1.9 constant_dynamic-slice_fusion.14
  224.9 1.9 constant_dynamic-slice_fusion.14
  229.8 1.9 constant_dynamic-slice_fusion.14
  234.8 1.9 constant_dynamic-slice_fusion.14
  239.7 1.9 constant_dynamic-slice_fusion.14
  244.7 1.9 constant_dynamic-slice_fusion.14
  249.6 1.9 constant_dynamic-slice_fusion.14
  254.6 1.9 constant_dynamic-slice_fusion.14
  259.5 1.9 constant_dynamic-slice_fusion.14
  264.5 1.9 constant_dynamic-slice_fusion.14
  269.4 1.9 constant_dynamic-slice_fusion.14
  274.4 1.9 constant_dynamic-slice_fusion.14
  279.3 1.9 constant_dynamic-slice_fusion.14
  284.3 1.9 constant_dynamic-slice_fusion.14
  289.2 1.9 constant_dynamic-slice_fusion.14
  294.2 1.9 constant_dynamic-slice_fusion.14
  299.1 1.9 constant_dynamic-slice_fusion.14
  304.1 1.9 constant_dynamic-slice_fusion.14
  309.0 1.9 constant_dynamic-slice_fusion.14
  314.0 1.9 constant_dynamic-slice_fusion.14
  318.9 1.9 constant_dynamic-slice_fusion.14
  323.9 1.9 constant_dynamic-slice_fusion.14
  328.8 1.9 constant_dynamic-slice_fusion.14
  333.8 1.9 constant_dynamic-slice_fusion.14
  338.7 1.9 constant_dynamic-slice_fusion.14
  343.7 1.9 constant_dynamic-slice_fusion.14
  348.6 1.9 constant_dynamic-slice_fusion.14
  354.1 39.5 %all-reduce = (f32[]{:T(128)}, f32[]{:T(128)}) all-reduce(f32[]{:T(128)} %get-tuple-element.589, f32[]{:T(128)} %get-tuple-element.588), channel_id=1, replica_groups=mesh['gx'=4,'gy'=4,'gz'=2] {'gx','gy','gz'}, use_global_device_ids=true, to_apply=%region_21.22 | all-reduce | flops 2 | bytes 16 | tf_op jit(solution)/shard_map/psum | solution.py:140
  (1218 shorter events, 179.7 us)
Async XLA Ops:
  2.2 0.9 copy-start
  49.3 2.1 copy-start.1
  49.5 1.8 copy-start.2
  49.5 8.9 %collective-permute-start.6 = (f32[6,1,2,2,128]{4,3,2,0,1:T(2,128)S(1)}, f32[6,1,2,2,128]{4,3,2,0,1:T(2,128)S(1)}, u32[]{:S(2)}, u32[]{:S(2)}) collective-permute-start(f32[6,1,2,2,128]{4,3,2,0,1:T(2,128)S(1)} %bitcast.219), channel_id=1, source_target_pairs={{0,8},{8,16},{16,24},{24,0},{1,9},{9,17},{17,25},{25,1},{2,10},{10... | collective-permute-start | bytes 36872 | tf_op jit(solution)/shard_map/ppermute | solution.py:19
  49.6 8.8 %collective-permute-start.7 = (f32[6,1,2,2,128]{4,3,2,0,1:T(2,128)S(1)}, f32[6,1,2,2,128]{4,3,2,0,1:T(2,128)S(1)}, u32[]{:S(2)}, u32[]{:S(2)}) collective-permute-start(f32[6,1,2,2,128]{4,3,2,0,1:T(2,128)S(1)} %bitcast.220), channel_id=1, source_target_pairs={{8,0},{16,8},{24,16},{0,24},{9,1},{17,9},{25,17},{1,25},{10,2},{18... | collective-permute-start | bytes 36872 | tf_op jit(solution)/shard_map/ppermute | solution.py:21
  51.3 1.8 copy-start.4
  51.4 3.1 collective-permute-start
  52.1 2.5 collective-permute-start.1
  53.2 0.7 copy-start.5
  54.6 7.8 %collective-permute-start.2 = (f32[4,3,1,2,128]{4,3,2,1,0:T(2,128)S(1)}, f32[4,3,1,2,128]{4,3,2,1,0:T(2,128)S(1)}, u32[]{:S(2)}, u32[]{:S(2)}) collective-permute-start(f32[4,3,1,2,128]{4,3,2,1,0:T(2,128)S(1)} %get-tuple-element.669), channel_id=1, source_target_pairs={{0,2},{2,4},{4,6},{6,0},{1,3},{3,5},{5,7},{7,1},{8,10},{10,12},{12... | collective-permute-start | bytes 36872 | tf_op jit(solution)/shard_map/ppermute | solution.py:19
  56.1 6.3 %collective-permute-start.3 = (f32[4,3,1,2,128]{4,3,2,1,0:T(2,128)S(1)}, f32[4,3,1,2,128]{4,3,2,1,0:T(2,128)S(1)}, u32[]{:S(2)}, u32[]{:S(2)}) collective-permute-start(f32[4,3,1,2,128]{4,3,2,1,0:T(2,128)S(1)} %get-tuple-element.670), channel_id=1, source_target_pairs={{2,0},{4,2},{6,4},{0,6},{3,1},{5,3},{7,5},{1,7},{10,8},{12,10},{14... | collective-permute-start | bytes 36872 | tf_op jit(solution)/shard_map/ppermute | solution.py:21
  58.5 6.4 %collective-permute-start.8 = (f32[6,3,1,2,128]{4,3,2,0,1:T(2,128)S(1)}, f32[6,3,1,2,128]{4,3,2,0,1:T(2,128)S(1)}, u32[]{:S(2)}, u32[]{:S(2)}) collective-permute-start(f32[6,3,1,2,128]{4,3,2,0,1:T(2,128)S(1)} %get-tuple-element.667), channel_id=1, source_target_pairs={{0,2},{2,4},{4,6},{6,0},{1,3},{3,5},{5,7},{7,1},{8,10},{10,12},{12... | collective-permute-start | bytes 55304 | tf_op jit(solution)/shard_map/ppermute | solution.py:19
  58.6 6.3 %collective-permute-start.9 = (f32[6,3,1,2,128]{4,3,2,0,1:T(2,128)S(1)}, f32[6,3,1,2,128]{4,3,2,0,1:T(2,128)S(1)}, u32[]{:S(2)}, u32[]{:S(2)}) collective-permute-start(f32[6,3,1,2,128]{4,3,2,0,1:T(2,128)S(1)} %get-tuple-element.668), channel_id=1, source_target_pairs={{2,0},{4,2},{6,4},{0,6},{3,1},{5,3},{7,5},{1,7},{10,8},{12,10},{14... | collective-permute-start | bytes 55304 | tf_op jit(solution)/shard_map/ppermute | solution.py:21
  62.4 4.6 %collective-permute-start.4 = (f32[4,3,4,1,128]{4,3,2,1,0:T(1,128)S(1)}, f32[4,3,4,1,128]{4,3,2,1,0:T(1,128)S(1)}, u32[]{:S(2)}, u32[]{:S(2)}) collective-permute-start(f32[4,3,4,1,128]{4,3,2,1,0:T(1,128)S(1)} %get-tuple-element.663), channel_id=1, source_target_pairs={{0,1},{1,0},{2,3},{3,2},{4,5},{5,4},{6,7},{7,6},{8,9},{9,8},{10,11... | collective-permute-start | bytes 73736 | tf_op jit(solution)/shard_map/ppermute | solution.py:19
  64.8 4.1 %collective-permute-start.5 = (f32[4,3,4,1,128]{4,3,2,1,0:T(1,128)S(1)}, f32[4,3,4,1,128]{4,3,2,1,0:T(1,128)S(1)}, u32[]{:S(2)}, u32[]{:S(2)}) collective-permute-start(f32[4,3,4,1,128]{4,3,2,1,0:T(1,128)S(1)} %get-tuple-element.664), channel_id=1, source_target_pairs={{1,0},{0,1},{3,2},{2,3},{5,4},{4,5},{7,6},{6,7},{9,8},{8,9},{11,10... | collective-permute-start | bytes 73736 | tf_op jit(solution)/shard_map/ppermute | solution.py:21
  65.0 4.4 %collective-permute-start.10 = (f32[6,3,4,1,128]{4,3,2,0,1:T(1,128)S(1)}, f32[6,3,4,1,128]{4,3,2,0,1:T(1,128)S(1)}, u32[]{:S(2)}, u32[]{:S(2)}) collective-permute-start(f32[6,3,4,1,128]{4,3,2,0,1:T(1,128)S(1)} %get-tuple-element.661), channel_id=1, source_target_pairs={{0,1},{1,0},{2,3},{3,2},{4,5},{5,4},{6,7},{7,6},{8,9},{9,8},{10,11... | collective-permute-start | bytes 110600 | tf_op jit(solution)/shard_map/ppermute | solution.py:19
  67.0 4.0 collective-permute-start.11
  71.1 134.4 %copy-start.3 = (f32[6,1,2,2,128]{4,3,2,1,0:T(2,128)S(1)}, f32[6,1,2,2,128]{4,3,2,1,0:T(2,128)}, u32[]{:S(2)}) copy-start(f32[6,1,2,2,128]{4,3,2,1,0:T(2,128)} %param.14) | copy-start | bytes 36868
  205.5 3.2 collective-permute-start.12
  205.6 3.1 collective-permute-start.13
  208.8 5.6 %collective-permute-start.14 = (f32[6,3,1,2,128]{4,3,2,1,0:T(2,128)S(1)}, f32[6,3,1,2,128]{4,3,2,1,0:T(2,128)S(1)}, u32[]{:S(2)}, u32[]{:S(2)}) collective-permute-start(f32[6,3,1,2,128]{4,3,2,1,0:T(2,128)S(1)} %get-tuple-element.665), channel_id=1, source_target_pairs={{0,2},{2,4},{4,6},{6,0},{1,3},{3,5},{5,7},{7,1},{8,10},{10,12},{12... | collective-permute-start | bytes 55304 | tf_op jit(solution)/shard_map/ppermute | solution.py:19
  208.8 5.6 %collective-permute-start.15 = (f32[6,3,1,2,128]{4,3,2,1,0:T(2,128)S(1)}, f32[6,3,1,2,128]{4,3,2,1,0:T(2,128)S(1)}, u32[]{:S(2)}, u32[]{:S(2)}) collective-permute-start(f32[6,3,1,2,128]{4,3,2,1,0:T(2,128)S(1)} %get-tuple-element.666), channel_id=1, source_target_pairs={{2,0},{4,2},{6,4},{0,6},{3,1},{5,3},{7,5},{1,7},{10,8},{12,10},{14... | collective-permute-start | bytes 55304 | tf_op jit(solution)/shard_map/ppermute | solution.py:21
  214.5 4.1 %collective-permute-start.16 = (f32[6,3,4,1,128]{4,3,2,1,0:T(1,128)S(1)}, f32[6,3,4,1,128]{4,3,2,1,0:T(1,128)S(1)}, u32[]{:S(2)}, u32[]{:S(2)}) collective-permute-start(f32[6,3,4,1,128]{4,3,2,1,0:T(1,128)S(1)} %get-tuple-element.659), channel_id=1, source_target_pairs={{0,1},{1,0},{2,3},{3,2},{4,5},{5,4},{6,7},{7,6},{8,9},{9,8},{10,11... | collective-permute-start | bytes 110600 | tf_op jit(solution)/shard_map/ppermute | solution.py:19
  215.0 4.1 %collective-permute-start.17 = (f32[6,3,4,1,128]{4,3,2,1,0:T(1,128)S(1)}, f32[6,3,4,1,128]{4,3,2,1,0:T(1,128)S(1)}, u32[]{:S(2)}, u32[]{:S(2)}) collective-permute-start(f32[6,3,4,1,128]{4,3,2,1,0:T(1,128)S(1)} %get-tuple-element.660), channel_id=1, source_target_pairs={{1,0},{0,1},{3,2},{2,3},{5,4},{4,5},{7,6},{6,7},{9,8},{8,9},{11,10... | collective-permute-start | bytes 110600 | tf_op jit(solution)/shard_map/ppermute | solution.py:21
where the time goes:
time: 398 us; the launch traced here: 396 us
  other arithmetic  220 us (55%)
  blocking collectives  81.5 us (20%)
  local copies, waits for them, and re-layouts  45.7 us (11%)
  starting transfers between devices  23.6 us (6%)
  loops' own time  10.9 us (3%)
  waiting for transfers between devices  9.95 us (2%)
    reduce_sum x108, other arithmetic, pair_field(): jnp.sum(radial * project * displace[axis_num] - direct * parts[axis_num],...  102 us
    slice x27, other arithmetic, pair_field(): moment[3 * which_set + axis_num][:, None, :]  52 us
    add x27, other arithmetic, pair_field(): offset_vec[axis_num] + source[axis_num][:, None, :]  51.6 us
    psum x1, blocking collectives, global_gram(): return lax.psum(local_gram, ('gx', 'gy', 'gz'))  42 us
    psum x1, blocking collectives, on_device(): lax.psum((jnp.sum(update * update), jnp.sum(induced * induced)), ('gx', '...  39.5 us
    slice x54, local copies, waits for them, and re-layouts, pair_field(): offset_vec[axis_num] + source[axis_num][:, None, :]  36 us
    ppermute x9, starting transfers between devices, with_halo(): lax.ppermute(head, axis, [((i + 1) % count, i) for i in range(count)])  16.3 us
    another operation x2, loops' own time, slab_field(): lax.fori_loop(0, 27, offset_step, jnp.zeros((rows, width_y * width_z, slo...  10.9 us
  transfers between devices with their start and end apart: 18, of which 8 were waited for; matrix products, arithmetic and copies ran while one was open for 0% of the time, Pallas kernels for 0%

commit v1 on v0

v1 whole, which is shorter than its diff:
```python
import functools

import jax
import jax.numpy as jnp
from jax import lax
from jax.experimental import pallas as pl
from jax.experimental.pallas import tpu as pltpu
from jax.sharding import PartitionSpec as P

CELL_EDGE = 10.0
SOFTENING = 0.3
THOLE_DAMP = 0.39
RELAXATION = 0.7
MESH = pl.DeviceIdType.MESH
AXES = ("gx", "gy", "gz")
ROWS = 8
BLOCK = 32


def halo_moves(devices, tiles):
    options = []
    for count, n in zip(devices, tiles):
        if count == 2 and n == 2:
            around = [(1, 0, 2, 2)]
        else:
            around = [(1, n - 1, 1, n + 1), (-1, 0, 1, n)]
        options.append([(0, 0, n, 0)] + around)
    return [
        (a, b, c) for a in options[0] for b in options[1] for c in options[2] if (a[0], b[0], c[0]) != (0, 0, 0)
    ]


def solve_fit(total, past, lane, pair_lane):
    def pick(a, b):
        index = pair_lane[(min(a, b), max(a, b))]
        return jnp.sum(jnp.where(lane == index, total, 0.0), axis=1, keepdims=True)

    diagonal = [pick(a, a) for a in range(past)]
    trace = diagonal[0]
    for value in diagonal[1:]:
        trace = trace + value
    ridge = 0.001 * trace / past + 1.0
    lower, inverse = {}, []
    for j in range(past):
        pivot = diagonal[j] + ridge
        for m in range(j):
            pivot = pivot - lower[j, m] * lower[j, m]
        inverse.append(1.0 / jnp.sqrt(pivot))
        for i in range(j + 1, past):
            value = pick(i, j)
            for m in range(j):
                value = value - lower[i, m] * lower[j, m]
            lower[i, j] = value * inverse[j]
    forward = []
    for i in range(past):
        value = pick(i, past)
        for m in range(i):
            value = value - lower[i, m] * forward[m]
        forward.append(value * inverse[i])
    coeffs = [None] * past
    for i in reversed(range(past)):
        value = forward[i]
        for m in range(i + 1, past):
            value = value - lower[m, i] * coeffs[m]
        coeffs[i] = value * inverse[i]
    return coeffs


def kernel(
    devices,
    frac_ref, pol_ref, occ_ref, mask_ref, perm_ref, hist_ref,
    out_ref, change_ref,
    geom, held_one, held_two, past_sets, own, radial, direct, sums, slots_a, slots_b,
    send_all, recv_all, send_geom, recv_geom, send_one, recv_one, send_two, recv_two,
):
    tiles = tuple(frac_ref.shape[1:4])
    slots = frac_ref.shape[4]
    steps = hist_ref.shape[0]
    rows = hist_ref.shape[1]
    past = steps - 1
    total_devices = devices[0] * devices[1] * devices[2]
    at = [lax.axis_index(axis) for axis in AXES]
    me = (at[0] * devices[1] + at[1]) * devices[2] + at[2]
    moves = halo_moves(devices, tiles)
    lane = lax.broadcasted_iota(jnp.int32, (1, slots), 1)

    def coords(index):
        return (index // (devices[1] * devices[2]), index // devices[2] % devices[1], index % devices[2])

    barrier = pltpu.get_barrier_semaphore()

    def greet(step, carry):
        pl.semaphore_signal(
            barrier, inc=1, device_id=coords((me + step) % total_devices), device_id_type=MESH
        )
        return carry

    lax.fori_loop(1, total_devices, greet, 0)

    def everyone(index, held):
        def one(step):
            return pltpu.make_async_remote_copy(
                src_ref=held.at[pl.ds(me, 1)],
                dst_ref=held.at[pl.ds(me, 1)],
                send_sem=send_all.at[index],
                recv_sem=recv_all.at[index],
                device_id=coords((me + step) % total_devices),
                device_id_type=MESH,
            )

        def start(step, carry):
            one(step).start()
            return carry

        lax.fori_loop(1, total_devices, start, 0)

    def everyone_wait(index, held):
        whole = pltpu.make_async_remote_copy(
            src_ref=held.at[pl.ds(0, total_devices - 1)],
            dst_ref=held.at[pl.ds(0, total_devices - 1)],
            send_sem=send_all.at[index],
            recv_sem=recv_all.at[index],
            device_id=coords((me + 1) % total_devices),
            device_id_type=MESH,
        )
        whole.wait_send()
        whole.wait_recv()

    def halo(held, send, recv):
        copies = []
        for number, move in enumerate(moves):
            source = tuple(pl.ds(part[1], part[2]) for part in move)
            place = tuple(pl.ds(part[3], part[2]) for part in move)
            target = tuple((at[axis] + move[axis][0] + devices[axis]) % devices[axis] for axis in range(3))
            copies.append(
                pltpu.make_async_remote_copy(
                    src_ref=held.at[source],
                    dst_ref=held.at[place],
                    send_sem=send.at[number],
                    recv_sem=recv.at[number],
                    device_id=target,
                    device_id_type=MESH,
                )
            )
        return copies

    places = [(x, y, z) for x in range(tiles[0]) for y in range(tiles[1]) for z in range(tiles[2])]
    zero_row = jnp.zeros((1, slots), jnp.float32)
    spare = jnp.zeros((ROWS - rows, slots), jnp.float32)
    filled, scaled, fixed = [], [], []
    for t, (x, y, z) in enumerate(places):
        full = occ_ref[x, y, z, :].reshape(1, slots).astype(jnp.float32)
        pol = pol_ref[x, y, z, :].reshape(1, slots)
        scaled.append(RELAXATION * full * pol)
        tile = jnp.concatenate(
            [frac_ref[c, x, y, z, :].reshape(1, slots) * CELL_EDGE for c in range(3)]
            + [lax.rsqrt(pol)] + [zero_row] * (ROWS - 4),
            axis=0,
        )
        geom[x, y, z] = tile
        for h in range(steps):
            moment = jnp.concatenate(
                [hist_ref[h, c, x, y, z, :].reshape(1, slots) for c in range(rows)], axis=0
            )
            past_sets[h, t] = jnp.concatenate([moment * full, spare], axis=0)
        fixed.append(
            jnp.concatenate(
                [perm_ref[c, x, y, z, :].reshape(1, slots) for c in range(rows)] + [spare], axis=0
            )
        )
    pair_lane = {}
    gram = zero_row
    for a in range(steps):
        for b in range(a, steps):
            product = past_sets[a, 0] * past_sets[b, 0]
            for t in range(1, len(places)):
                product = product + past_sets[a, t] * past_sets[b, t]
            value = jnp.sum(jnp.sum(product, axis=0, keepdims=True), axis=1, keepdims=True)
            pair_lane[(a, b)] = len(pair_lane)
            gram = jnp.where(lane == pair_lane[(a, b)], value, gram)
    slots_a[pl.ds(me, 1)] = gram.reshape(1, 1, slots)

    pl.semaphore_wait(barrier, total_devices - 1)
    geom_copies = halo(geom, send_geom, recv_geom)
    everyone(0, slots_a)
    for copy in geom_copies:
        copy.start()

    for t, (x, y, z) in enumerate(places):
        for c in range(4):
            row = geom[x, y, z, c, :].reshape(1, slots)
            own[t, c] = jnp.broadcast_to(row, (slots, slots)).T

    everyone_wait(0, slots_a)
    total = jnp.sum(slots_a[...], axis=0)
    coeffs = solve_fit(total, past, lane, pair_lane)
    for t, (x, y, z) in enumerate(places):
        value = coeffs[0] * past_sets[1, t]
        for h in range(1, past):
            value = value + coeffs[h] * past_sets[h + 1, t]
        held_one[x, y, z] = value
    one_copies = halo(held_one, send_one, recv_one)
    for copy in one_copies:
        copy.start()
    for copy in geom_copies:
        copy.wait()

    wraps = tuple(n + 2 for n in tiles)

    def wrap(value, size):
        return jnp.where(value < 0, value + size, value)

    def spot(t, along):
        x = t // (tiles[1] * tiles[2])
        y = t // tiles[2] % tiles[1]
        z = t % tiles[2]
        return (x, y, z)

    def source_rows(held, place, names):
        return [held[place[0], place[1], place[2], pl.ds(c, 1), :] for c in names]

    def geometry(step, carry):
        t, k = step // 27, step % 27
        along = (k // 9 - 1, k // 3 % 3 - 1, k % 3 - 1)
        base = spot(t, along)
        place = tuple(wrap(base[i] + along[i], wraps[i]) for i in range(3))
        source = source_rows(geom, place, range(4))
        for i in range(3):
            source[i] = source[i] + CELL_EDGE * along[i].astype(jnp.float32)
        damp = source[3] * THOLE_DAMP
        allowed = mask_ref[base[0], base[1], base[2], k].astype(jnp.float32)
        for first in range(0, slots, BLOCK):
            part = pl.ds(first, BLOCK)
            dx = source[0] - own[t, 0, part, :]
            dy = source[1] - own[t, 1, part, :]
            dz = source[2] - own[t, 2, part, :]
            square = dx * dx + dy * dy + dz * dz + SOFTENING
            root = lax.rsqrt(square)
            root_two = root * root
            cube = root_two * root * allowed
            arg = (square * square) * root * (damp * own[t, 3, part, :])
            fade = jnp.exp(-arg)
            three = 1.0 - fade
            five = three - arg * fade
            direct[t, k, part, :] = three * cube
            radial[t, k, part, :] = five * cube * (3.0 * root_two)
        return carry

    count = len(places)
    lax.fori_loop(0, count * 27, geometry, 0)
    off_diagonal = lax.broadcasted_iota(jnp.int32, (slots, slots), 0) != lax.broadcasted_iota(
        jnp.int32, (slots, slots), 1
    )
    for t in range(count):
        direct[t, 13] = jnp.where(off_diagonal, direct[t, 13], 0.0)
        radial[t, 13] = jnp.where(off_diagonal, radial[t, 13], 0.0)

    ones = jnp.ones((ROWS, slots), jnp.float32)
    blocks = slots // BLOCK

    def field(held):
        def block_step(step, carry):
            t, part_index = step // blocks, step % blocks
            part = pl.ds(pl.multiple_of(part_index * BLOCK, BLOCK), BLOCK)
            base = spot(t, None)
            target = [own[t, c, part, :] for c in range(3)]

            def offsets(nine, acc):
                along_x, along_y = nine // 3 - 1, nine % 3 - 1
                acc = list(acc)
                for along_z in (-1, 0, 1):
                    along = (along_x, along_y, along_z)
                    place = tuple(wrap(base[i] + along[i], wraps[i]) for i in range(3))
                    source = source_rows(geom, place, range(3))
                    moment = source_rows(held, place, range(rows))
                    k = nine * 3 + along_z + 1
                    r = radial[t, k, part, :]
                    d = direct[t, k, part, :]
                    shift = [
                        CELL_EDGE * along_x.astype(jnp.float32),
                        CELL_EDGE * along_y.astype(jnp.float32),
                        CELL_EDGE * along_z,
                    ]
                    apart = [(source[i] + shift[i]) - target[i] for i in range(3)]
                    for s in range(rows // 3):
                        m = moment[3 * s : 3 * s + 3]
                        project = (apart[0] * m[0] + apart[1] * m[1] + apart[2] * m[2]) * r
                        for i in range(3):
                            acc[3 * s + i] = acc[3 * s + i] + (project * apart[i] - d * m[i])
                return tuple(acc)

            acc = lax.fori_loop(
                0, 9, offsets, tuple(jnp.zeros((BLOCK, slots), jnp.float32) for _ in range(rows))
            )
            for c in range(rows):
                sums[t, c, part, :] = acc[c]
            return carry

        lax.fori_loop(0, count * blocks, block_step, 0)
        fields = []
        for t in range(count):
            parts = [
                lax.dot_general(
                    ones, sums[t, c], (((1,), (1,)), ((), ())),
                    precision=lax.Precision.HIGHEST, preferred_element_type=jnp.float32,
                )[0:1]
                for c in range(rows)
            ]
            fields.append(jnp.concatenate(parts + [spare], axis=0))
        return fields

    for copy in one_copies:
        copy.wait()
    fields = field(held_one)
    for t, (x, y, z) in enumerate(places):
        held_two[x, y, z] = (1.0 - RELAXATION) * held_one[x, y, z] + scaled[t] * (fixed[t] + fields[t])
    two_copies = halo(held_two, send_two, recv_two)
    for copy in two_copies:
        copy.start()
    for copy in two_copies:
        copy.wait()
    fields = field(held_two)
    changed = jnp.zeros((ROWS, slots), jnp.float32)
    size = jnp.zeros((ROWS, slots), jnp.float32)
    for t, (x, y, z) in enumerate(places):
        before = held_two[x, y, z]
        after = (1.0 - RELAXATION) * before + scaled[t] * (fixed[t] + fields[t])
        for c in range(rows):
            out_ref[c, x, y, z, :] = after[c]
        changed = changed + (after - before) * (after - before)
        size = size + after * after

    def all_of(value):
        return jnp.sum(jnp.sum(value, axis=0, keepdims=True), axis=1, keepdims=True)

    pair = jnp.where(lane == 0, all_of(changed), jnp.where(lane == 1, all_of(size), 0.0))
    slots_b[pl.ds(me, 1)] = pair.reshape(1, 1, slots)
    everyone(1, slots_b)
    everyone_wait(1, slots_b)
    pair = jnp.sum(slots_b[...], axis=0)
    above = jnp.sum(jnp.where(lane == 0, pair, 0.0), axis=1, keepdims=True)
    below = jnp.sum(jnp.where(lane == 1, pair, 0.0), axis=1, keepdims=True)
    change_ref[...] = jnp.broadcast_to(jnp.sqrt(above / (below + 1.0)), (1, slots))


def solution(mesh):
    devices = tuple(mesh.shape[axis] for axis in AXES)
    total_devices = devices[0] * devices[1] * devices[2]

    def on_device(fractions, polarizability, occupancy, pair_mask, perm_field, history):
        tiles = fractions.shape[1:4]
        slots = fractions.shape[4]
        count = tiles[0] * tiles[1] * tiles[2]
        wraps = tuple(n + 2 for n in tiles)
        moves = len(halo_moves(devices, tiles))
        rows = history.shape[1]
        vmem = pl.BlockSpec(memory_space=pltpu.VMEM)
        smem = pl.BlockSpec(memory_space=pltpu.SMEM)
        f32 = jnp.float32
        induced, change = pl.pallas_call(
            functools.partial(kernel, devices),
            out_shape=(
                jax.ShapeDtypeStruct(perm_field.shape, f32),
                jax.ShapeDtypeStruct((1, slots), f32),
            ),
            in_specs=[vmem, vmem, vmem, smem, vmem, vmem],
            out_specs=(vmem, vmem),
            scratch_shapes=[
                pltpu.VMEM(wraps + (ROWS, slots), f32),
                pltpu.VMEM(wraps + (ROWS, slots), f32),
                pltpu.VMEM(wraps + (ROWS, slots), f32),
                pltpu.VMEM((history.shape[0], count, ROWS, slots), f32),
                pltpu.VMEM((count, 4, slots, slots), f32),
                pltpu.VMEM((count, 27, slots, slots), f32),
                pltpu.VMEM((count, 27, slots, slots), f32),
                pltpu.VMEM((count, rows, slots, slots), f32),
                pltpu.VMEM((total_devices, 1, slots), f32),
                pltpu.VMEM((total_devices, 1, slots), f32),
                pltpu.SemaphoreType.DMA((2,)),
                pltpu.SemaphoreType.DMA((2,)),
            ]
            + [pltpu.SemaphoreType.DMA((moves,))] * 6,
            compiler_params=pltpu.CompilerParams(
                collective_id=0, has_side_effects=True, vmem_limit_bytes=40 * 1024 * 1024
            ),
        )(fractions, polarizability, occupancy, pair_mask, perm_field, history)
        return induced, change[0, 0]

    in_specs = (
        P(None, "gx", "gy", "gz", None),
        P("gx", "gy", "gz", None),
        P("gx", "gy", "gz", None),
        P("gx", "gy", "gz", None),
        P(None, "gx", "gy", "gz", None),
        P(None, None, "gx", "gy", "gz", None),
    )
    out_specs = (P(None, "gx", "gy", "gz", None), P())
    return jax.shard_map(
        on_device, mesh=mesh, in_specs=in_specs, out_specs=out_specs, check_vma=False
    )
```

time: 398 us -> 73.3 us (0.18)
  other arithmetic: 220 us -> 0 us
  blocking collectives: 81.5 us -> 0 us
  Pallas kernels: 0 us -> 66.2 us
  local copies, waits for them, and re-layouts: 45.7 us -> 4.92 us
  starting transfers between devices: 23.6 us -> 0 us
  loops' own time: 10.9 us -> 0 us
  waiting for transfers between devices: 9.95 us -> 0 us
    reduce_sum x110 -> x0, other arithmetic: 104 us -> none  [the longest x108 102 us: pair_field(): jnp.sum(radial * project * displace[axis_num] - direct * parts[axis_num],...]
    psum x2 -> x0, blocking collectives: 81.5 us -> none  [the longest x1 42 us: global_gram(): return lax.psum(local_gram, ('gx', 'gy', 'gz'))]
    pallas_call x0 -> x1, Pallas kernels: none -> 66.2 us  [on_device(): pl.pallas_call(functools.partial(kernel, devices), out_shape=(jax.ShapeDt...]
    add x83 -> x0, other arithmetic: 52.3 us -> none  [the longest x27 51.6 us: pair_field(): offset_vec[axis_num] + source[axis_num][:, None, :]]
    slice x27 -> x0, other arithmetic: 52 us -> none  [pair_field(): moment[3 * which_set + axis_num][:, None, :]]
    slice x87 -> x0, local copies, waits for them, and re-layouts: 36.4 us -> none  [the longest x54 36 us: pair_field(): offset_vec[axis_num] + source[axis_num][:, None, :]]
    ppermute x18 -> x0, starting transfers between devices: 23.6 us -> none  [the longest x9 16.3 us: with_halo(): lax.ppermute(head, axis, [((i + 1) % count, i) for i in range(count)])]
    another operation x2 -> x0, loops' own time: 10.9 us -> none  [slab_field(): lax.fori_loop(0, 27, offset_step, jnp.zeros((rows, width_y * width_z, slo...]
  transfers between devices with their start and end apart: 18 -> 0, of which waited for: 8 -> 0; matrix products, arithmetic and copies ran while one was open for 0% -> 0% of each run, Pallas kernels for 0% -> 0%
where the time goes in v1:
time: 73.3 us; the launch traced here: 73 us
  Pallas kernels  66.2 us (90%)
  local copies, waits for them, and re-layouts  4.92 us (7%)
  between operations  1.82 us (2%)
    pallas_call x1, Pallas kernels, on_device(): pl.pallas_call(functools.partial(kernel, devices), out_shape=(jax.ShapeDt...  66.2 us
    unnamed x13, local copies, waits for them, and re-layouts  4.92 us

profile of v1, /device:TPU:0, one launch (start us, length us, event | category | flops | bytes accessed | tf_op | source)
XLA Modules:
  0.0 73.0 jit_solution(7848104016927112111)
XLA Ops:
  0.6 0.0 copy-start
  0.6 0.9 %copy-done = f32[6,6,1,2,2,128]{5,4,3,2,1,0:T(2,128)S(1)} copy-done((f32[6,6,1,2,2,128]{5,4,3,2,1,0:T(2,128)S(1)}, f32[6,6,1,2,2,128]{5,4,3,2,1,0:T(2,128)}, u32[]{:S(2)}) %copy-start) | copy-done | bytes 73752
  1.5 0.0 copy-start.1
  1.5 0.7 copy-done.1
  2.2 0.0 copy-start.2
  2.2 0.7 copy-done.2
  2.9 0.0 copy-start.3
  2.9 0.7 copy-done.3
  3.6 0.0 copy-start.4
  3.6 0.7 copy-done.4
  4.3 0.0 copy-start.5
  4.3 0.7 copy-done.5
  5.0 66.2 %shard_map.77 = (f32[6,1,2,2,128]{4,3,2,1,0:T(2,128)S(1)}, f32[1,128]{1,0:T(1,128)S(1)}) custom-call(f32[3,1,2,2,128]{4,3,2,1,0:T(2,128)S(1)} %copy-done.2, f32[1,2,2,128]{3,2,1,0:T(2,128)S(1)} %copy-done.3, s32[1,2,2,128]{3,2,1,0:T(2,128)S(1)} %copy-done.4, s32[1,2,2,27]{3,2,1,0:T(2,128)S(1)} %copy-done.5, f32[6,1,2,2,128]{4,3,2,1,0:T(2,128)S(1)} %copy-done.1, ...), custom_call_target="tpu_custom_call" | custom-call | tf_op jit(solution)/shard_map/pallas_call | solution.py:360
  71.2 0.6 copy.10
Async XLA Ops:
  0.6 0.9 %copy-start = (f32[6,6,1,2,2,128]{5,4,3,2,1,0:T(2,128)S(1)}, f32[6,6,1,2,2,128]{5,4,3,2,1,0:T(2,128)}, u32[]{:S(2)}) copy-start(f32[6,6,1,2,2,128]{5,4,3,2,1,0:T(2,128)} %hist_ref.1) | copy-start | bytes 221188
  1.5 0.7 copy-start.1
  2.2 0.7 copy-start.2
  2.9 0.7 copy-start.3
  3.6 0.7 copy-start.4
  4.3 0.7 copy-start.5

commit v2 on v1

--- a/solution.py
+++ b/solution.py
@@ -15,6 +15,7 @@
 AXES = ("gx", "gy", "gz")
 ROWS = 8
 BLOCK = 32
+FIELD_BLOCK = 32
 
 
 def halo_moves(devices, tiles):
@@ -27,6 +28,23 @@
         options.append([(0, 0, n, 0)] + around)
     return [
         (a, b, c) for a in options[0] for b in options[1] for c in options[2] if (a[0], b[0], c[0]) != (0, 0, 0)
+    ]
+
+
+def row_moves(devices, tiles, row):
+    along_x, along_y, along_z = [
+        [(0, 0, n, 0)] + [move[axis] for move in halo_moves(devices, tiles) if move[axis][0] != 0]
+        for axis, n in enumerate(tiles)
+    ]
+    n = tiles[1]
+    rows = [(0, row, 1, row)]
+    if row == n - 1:
+        rows.append((1, row, 1, n + 1))
+    if row == 0:
+        rows.append((-1, row, 1, n))
+    along_x, along_z = list(dict.fromkeys(along_x)), list(dict.fromkeys(along_z))
+    return [
+        (a, b, c) for a in along_x for b in rows for c in along_z if (a[0], b[0], c[0]) != (0, 0, 0)
     ]
 
 
@@ -68,10 +86,11 @@
 
 def kernel(
     devices,
+    frac_in, pol_in, occ_in, mask_in, perm_in, hist_in,
+    out_ref, change_ref,
     frac_ref, pol_ref, occ_ref, mask_ref, perm_ref, hist_ref,
-    out_ref, change_ref,
     geom, held_one, held_two, past_sets, own, radial, direct, sums, slots_a, slots_b,
-    send_all, recv_all, send_geom, recv_geom, send_one, recv_one, send_two, recv_two,
+    load_sem, send_all, recv_all, send_geom, recv_geom, send_one, recv_one, send_two, recv_two,
 ):
     tiles = tuple(frac_ref.shape[1:4])
     slots = frac_ref.shape[4]
@@ -83,6 +102,17 @@
     me = (at[0] * devices[1] + at[1]) * devices[2] + at[2]
     moves = halo_moves(devices, tiles)
     lane = lax.broadcasted_iota(jnp.int32, (1, slots), 1)
+    loads = [
+        pltpu.make_async_copy(source, target, load_sem.at[number])
+        for number, (source, target) in enumerate(
+            (
+                (hist_in, hist_ref), (occ_in, occ_ref), (frac_in, frac_ref),
+                (pol_in, pol_ref), (perm_in, perm_ref), (mask_in, mask_ref),
+            )
+        )
+    ]
+    for load in loads:
+        load.start()
 
     def coords(index):
         return (index // (devices[1] * devices[2]), index // devices[2] % devices[1], index % devices[2])
@@ -96,6 +126,8 @@
         return carry
 
     lax.fori_loop(1, total_devices, greet, 0)
+    for load in loads:
+        load.wait()
 
     def everyone(index, held):
         def one(step):
@@ -126,7 +158,7 @@
         whole.wait_send()
         whole.wait_recv()
 
-    def halo(held, send, recv):
+    def halo(held, send, recv, moves=moves):
         copies = []
         for number, move in enumerate(moves):
             source = tuple(pl.ds(part[1], part[2]) for part in move)
@@ -180,16 +212,73 @@
             gram = jnp.where(lane == pair_lane[(a, b)], value, gram)
     slots_a[pl.ds(me, 1)] = gram.reshape(1, 1, slots)
 
+    for t, (x, y, z) in enumerate(places):
+        for c in range(4):
+            row = geom[x, y, z, c, :].reshape(1, slots)
+            own[t, c] = jnp.broadcast_to(row, (slots, slots)).T
+
     pl.semaphore_wait(barrier, total_devices - 1)
     geom_copies = halo(geom, send_geom, recv_geom)
     everyone(0, slots_a)
     for copy in geom_copies:
         copy.start()
 
-    for t, (x, y, z) in enumerate(places):
-        for c in range(4):
-            row = geom[x, y, z, c, :].reshape(1, slots)
-            own[t, c] = jnp.broadcast_to(row, (slots, slots)).T
+    def clear(step, carry):
+        sums[step] = jnp.zeros((rows, slots, slots), jnp.float32)
+        return carry
+
+    lax.fori_loop(0, 2 * len(places), clear, 0)
+    for copy in geom_copies:
+        copy.wait()
+
+    wraps = tuple(n + 2 for n in tiles)
+
+    def wrap(value, size):
+        return jnp.where(value < 0, value + size, value)
+
+    def spot(t):
+        x = t // (tiles[1] * tiles[2])
+        y = t // tiles[2] % tiles[1]
+        z = t % tiles[2]
+        return (x, y, z)
+
+    def source_rows(held, place, names):
+        return [held[place[0], place[1], place[2], pl.ds(c, 1), :] for c in names]
+
+    def geometry(step, carry):
+        t, nine = step // 9, step % 9
+        along_x, along_y = nine // 3 - 1, nine % 3 - 1
+        base = spot(t)
+        for along_z in (-1, 0, 1):
+            along = (along_x, along_y, along_z)
+            k = nine * 3 + along_z + 1
+            place = tuple(wrap(base[i] + along[i], wraps[i]) for i in range(3))
+            source = source_rows(geom, place, range(4))
+            source[0] = source[0] + CELL_EDGE * along_x.astype(jnp.float32)
+            source[1] = source[1] + CELL_EDGE * along_y.astype(jnp.float32)
+            source[2] = source[2] + CELL_EDGE * along_z
+            damp = source[3] * THOLE_DAMP
+            allowed = mask_ref[base[0], base[1], base[2], k].astype(jnp.float32)
+            for first in range(0, slots, BLOCK):
+                part = pl.ds(first, BLOCK)
+                dx = source[0] - own[t, 0, part, :]
+                dy = source[1] - own[t, 1, part, :]
+                dz = source[2] - own[t, 2, part, :]
+                square = dx * dx + dy * dy + dz * dz + SOFTENING
+                root = lax.rsqrt(square)
+                root_two = root * root
+                cube = root_two * root * allowed
+                arg = (square * square) * root * (damp * own[t, 3, part, :])
+                fade = jnp.exp(-arg)
+                three = 1.0 - fade
+                five = three - arg * fade
+                direct[t, k, part, :] = three * cube
+                radial[t, k, part, :] = five * cube * (3.0 * root_two)
+        return carry
+
+    count = len(places)
+    early = count * 9 // 3
+    lax.fori_loop(0, early, geometry, 0)
 
     everyone_wait(0, slots_a)
     total = jnp.sum(slots_a[...], axis=0)
@@ -202,52 +291,7 @@
     one_copies = halo(held_one, send_one, recv_one)
     for copy in one_copies:
         copy.start()
-    for copy in geom_copies:
-        copy.wait()
-
-    wraps = tuple(n + 2 for n in tiles)
-
-    def wrap(value, size):
-        return jnp.where(value < 0, value + size, value)
-
-    def spot(t, along):
-        x = t // (tiles[1] * tiles[2])
-        y = t // tiles[2] % tiles[1]
-        z = t % tiles[2]
-        return (x, y, z)
-
-    def source_rows(held, place, names):
-        return [held[place[0], place[1], place[2], pl.ds(c, 1), :] for c in names]
-
-    def geometry(step, carry):
-        t, k = step // 27, step % 27
-        along = (k // 9 - 1, k // 3 % 3 - 1, k % 3 - 1)
-        base = spot(t, along)
-        place = tuple(wrap(base[i] + along[i], wraps[i]) for i in range(3))
-        source = source_rows(geom, place, range(4))
-        for i in range(3):
-            source[i] = source[i] + CELL_EDGE * along[i].astype(jnp.float32)
-        damp = source[3] * THOLE_DAMP
-        allowed = mask_ref[base[0], base[1], base[2], k].astype(jnp.float32)
-        for first in range(0, slots, BLOCK):
-            part = pl.ds(first, BLOCK)
-            dx = source[0] - own[t, 0, part, :]
-            dy = source[1] - own[t, 1, part, :]
-            dz = source[2] - own[t, 2, part, :]
-            square = dx * dx + dy * dy + dz * dz + SOFTENING
-            root = lax.rsqrt(square)
-            root_two = root * root
-            cube = root_two * root * allowed
-            arg = (square * square) * root * (damp * own[t, 3, part, :])
-            fade = jnp.exp(-arg)
-            three = 1.0 - fade
-            five = three - arg * fade
-            direct[t, k, part, :] = three * cube
-            radial[t, k, part, :] = five * cube * (3.0 * root_two)
-        return carry
-
-    count = len(places)
-    lax.fori_loop(0, count * 27, geometry, 0)
+    lax.fori_loop(early, count * 9, geometry, 0)
     off_diagonal = lax.broadcasted_iota(jnp.int32, (slots, slots), 0) != lax.broadcasted_iota(
         jnp.int32, (slots, slots), 1
     )
@@ -255,71 +299,90 @@
         direct[t, 13] = jnp.where(off_diagonal, direct[t, 13], 0.0)
         radial[t, 13] = jnp.where(off_diagonal, radial[t, 13], 0.0)
 
-    ones = jnp.ones((ROWS, slots), jnp.float32)
-    blocks = slots // BLOCK
-
-    def field(held):
-        def block_step(step, carry):
-            t, part_index = step // blocks, step % blocks
-            part = pl.ds(pl.multiple_of(part_index * BLOCK, BLOCK), BLOCK)
-            base = spot(t, None)
-            target = [own[t, c, part, :] for c in range(3)]
-
-            def offsets(nine, acc):
-                along_x, along_y = nine // 3 - 1, nine % 3 - 1
-                acc = list(acc)
-                for along_z in (-1, 0, 1):
-                    along = (along_x, along_y, along_z)
-                    place = tuple(wrap(base[i] + along[i], wraps[i]) for i in range(3))
-                    source = source_rows(geom, place, range(3))
-                    moment = source_rows(held, place, range(rows))
-                    k = nine * 3 + along_z + 1
-                    r = radial[t, k, part, :]
-                    d = direct[t, k, part, :]
-                    shift = [
-                        CELL_EDGE * along_x.astype(jnp.float32),
-                        CELL_EDGE * along_y.astype(jnp.float32),
-                        CELL_EDGE * along_z,
-                    ]
-                    apart = [(source[i] + shift[i]) - target[i] for i in range(3)]
-                    for s in range(rows // 3):
-                        m = moment[3 * s : 3 * s + 3]
-                        project = (apart[0] * m[0] + apart[1] * m[1] + apart[2] * m[2]) * r
-                        for i in range(3):
-                            acc[3 * s + i] = acc[3 * s + i] + (project * apart[i] - d * m[i])
-                return tuple(acc)
-
-            acc = lax.fori_loop(
-                0, 9, offsets, tuple(jnp.zeros((BLOCK, slots), jnp.float32) for _ in range(rows))
-            )
-            for c in range(rows):
-                sums[t, c, part, :] = acc[c]
+    blocks = slots // FIELD_BLOCK
+
+    def add_sources(held, index, step, base, along_y):
+        part = pl.ds(pl.multiple_of(step % blocks * FIELD_BLOCK, FIELD_BLOCK), FIELD_BLOCK)
+        t = (base[0] * tiles[1] + base[1]) * tiles[2] + base[2]
+        place_y = wrap(base[1] + along_y, wraps[1])
+        target = [own[t, c, part, :] for c in range(3)]
+        target[1] = target[1] - CELL_EDGE * along_y.astype(jnp.float32)
+        deep = [target[2] - CELL_EDGE * along_z for along_z in (-1, 0, 1)]
+
+        def plane(along_x, acc):
+            acc = list(acc)
+            place_x = wrap(base[0] + along_x, wraps[0])
+            wide = target[0] - CELL_EDGE * along_x
+            for along_z in (-1, 0, 1):
+                place = (place_x, place_y, wrap(base[2] + along_z, wraps[2]))
+                source = source_rows(geom, place, range(3))
+                moment = source_rows(held, place, range(rows))
+                k = 9 * (along_x + 1) + 3 * (along_y + 1) + along_z + 1
+                r = radial[t, k, part, :]
+                d = direct[t, k, part, :]
+                apart = [source[0] - wide, source[1] - target[1], source[2] - deep[along_z + 1]]
+                for s in range(rows // 3):
+                    m = moment[3 * s : 3 * s + 3]
+                    project = (apart[0] * m[0] + apart[1] * m[1] + apart[2] * m[2]) * r
+                    for i in range(3):
+                        acc[3 * s + i] = acc[3 * s + i] + (project * apart[i] - d * m[i])
+            return tuple(acc)
+
+        acc = tuple(sums[index * count + t, c, part, :] for c in range(rows))
+        for along_x in (-1, 0, 1):
+            acc = plane(along_x, acc)
+        for c in range(rows):
+            sums[index * count + t, c, part, :] = acc[c]
+
+    flat = tiles[0] * tiles[2] * blocks
+
+    def to_row(held, index, row):
+        def one(step, carry):
+            column = step // blocks % (tiles[0] * tiles[2])
+            base = (column // tiles[2], row, column % tiles[2])
+            add_sources(held, index, step, base, step // flat - 1)
             return carry
 
-        lax.fori_loop(0, count * blocks, block_step, 0)
-        fields = []
-        for t in range(count):
-            parts = [
-                lax.dot_general(
-                    ones, sums[t, c], (((1,), (1,)), ((), ())),
-                    precision=lax.Precision.HIGHEST, preferred_element_type=jnp.float32,
-                )[0:1]
-                for c in range(rows)
-            ]
-            fields.append(jnp.concatenate(parts + [spare], axis=0))
-        return fields
+        lax.fori_loop(0, 3 * flat, one, 0)
+
+    def from_row(held, index, row):
+        def one(step, carry):
+            column = step // blocks % (tiles[0] * tiles[2])
+            along_y = step // flat - 1
+            base = (column // tiles[2], (row - along_y + tiles[1]) % tiles[1], column % tiles[2])
+            add_sources(held, index, step, base, along_y)
+            return carry
+
+        lax.fori_loop(0, 3 * flat, one, 0)
+
+    square_lane = lax.broadcasted_iota(jnp.int32, (slots, slots), 1)
+
+    def field_of(index, t):
+        columns = jnp.zeros((slots, slots), jnp.float32)
+        for c in range(rows):
+            value = jnp.sum(sums[index * count + t, c], axis=1, keepdims=True)
+            columns = jnp.where(square_lane == c, value, columns)
+        return columns.T[0:ROWS]
 
     for copy in one_copies:
         copy.wait()
-    fields = field(held_one)
-    for t, (x, y, z) in enumerate(places):
-        held_two[x, y, z] = (1.0 - RELAXATION) * held_one[x, y, z] + scaled[t] * (fixed[t] + fields[t])
-    two_copies = halo(held_two, send_two, recv_two)
-    for copy in two_copies:
-        copy.start()
-    for copy in two_copies:
-        copy.wait()
-    fields = field(held_two)
+    two_copies = []
+    for row in range(tiles[1]):
+        to_row(held_one, 0, row)
+        for t, (x, y, z) in enumerate(places):
+            if y == row:
+                held_two[x, y, z] = (1.0 - RELAXATION) * held_one[x, y, z] + scaled[t] * (
+                    fixed[t] + field_of(0, t)
+                )
+        copies = halo(held_two, send_two.at[row], recv_two.at[row], row_moves(devices, tiles, row))
+        for copy in copies:
+            copy.start()
+        two_copies.append(copies)
+    for row in range(tiles[1]):
+        for copy in two_copies[row]:
+            copy.wait()
+        from_row(held_two, 1, row)
+    fields = [field_of(1, t) for t in range(count)]
     changed = jnp.zeros((ROWS, slots), jnp.float32)
     size = jnp.zeros((ROWS, slots), jnp.float32)
     for t, (x, y, z) in enumerate(places):
@@ -355,7 +418,6 @@
         moves = len(halo_moves(devices, tiles))
         rows = history.shape[1]
         vmem = pl.BlockSpec(memory_space=pltpu.VMEM)
-        smem = pl.BlockSpec(memory_space=pltpu.SMEM)
         f32 = jnp.float32
         induced, change = pl.pallas_call(
             functools.partial(kernel, devices),
@@ -363,9 +425,15 @@
                 jax.ShapeDtypeStruct(perm_field.shape, f32),
                 jax.ShapeDtypeStruct((1, slots), f32),
             ),
-            in_specs=[vmem, vmem, vmem, smem, vmem, vmem],
+            in_specs=[pl.BlockSpec(memory_space=pltpu.HBM)] * 6,
             out_specs=(vmem, vmem),
             scratch_shapes=[
+                pltpu.VMEM(fractions.shape, f32),
+                pltpu.VMEM(polarizability.shape, f32),
+                pltpu.VMEM(occupancy.shape, jnp.int32),
+                pltpu.SMEM(pair_mask.shape, jnp.int32),
+                pltpu.VMEM(perm_field.shape, f32),
+                pltpu.VMEM(history.shape, f32),
                 pltpu.VMEM(wraps + (ROWS, slots), f32),
                 pltpu.VMEM(wraps + (ROWS, slots), f32),
                 pltpu.VMEM(wraps + (ROWS, slots), f32),
@@ -373,15 +441,17 @@
                 pltpu.VMEM((count, 4, slots, slots), f32),
                 pltpu.VMEM((count, 27, slots, slots), f32),
                 pltpu.VMEM((count, 27, slots, slots), f32),
-                pltpu.VMEM((count, rows, slots, slots), f32),
+                pltpu.VMEM((2 * count, rows, slots, slots), f32),
                 pltpu.VMEM((total_devices, 1, slots), f32),
                 pltpu.VMEM((total_devices, 1, slots), f32),
+                pltpu.SemaphoreType.DMA((6,)),
                 pltpu.SemaphoreType.DMA((2,)),
                 pltpu.SemaphoreType.DMA((2,)),
             ]
-            + [pltpu.SemaphoreType.DMA((moves,))] * 6,
+            + [pltpu.SemaphoreType.DMA((moves,))] * 4
+            + [pltpu.SemaphoreType.DMA((tiles[1], moves))] * 2,
             compiler_params=pltpu.CompilerParams(
-                collective_id=0, has_side_effects=True, vmem_limit_bytes=40 * 1024 * 1024
+                collective_id=0, has_side_effects=True, vmem_limit_bytes=67043328
             ),
         )(fractions, polarizability, occupancy, pair_mask, perm_field, history)
         return induced, change[0, 0]

time: 73.3 us -> 59.9 us (0.82)
  Pallas kernels: 66.2 us -> 56.6 us
  local copies, waits for them, and re-layouts: 4.92 us -> 1.31 us
    pallas_call x1, Pallas kernels: 66.2 us -> 56.6 us  [on_device(): pl.pallas_call(functools.partial(kernel, devices), out_shape=(jax.ShapeDt...]
    unnamed x13 -> x3, local copies, waits for them, and re-layouts: 4.92 us -> 1.31 us
where the time goes in v2:
time: 59.9 us; the launch traced here: 59.7 us
  Pallas kernels  56.6 us (94%)
  between operations  1.81 us (3%)
  local copies, waits for them, and re-layouts  1.31 us (2%)
    pallas_call x1, Pallas kernels, on_device(): pl.pallas_call(functools.partial(kernel, devices), out_shape=(jax.ShapeDt...  56.6 us
    unnamed x3, local copies, waits for them, and re-layouts  1.31 us

profile of v2, /device:TPU:0, one launch (start us, length us, event | category | flops | bytes accessed | tf_op | source)
XLA Modules:
  0.0 59.7 jit_solution(5248839918024811043)
XLA Ops:
  0.6 56.6 %shard_map.77 = (f32[6,1,2,2,128]{4,3,2,1,0:T(2,128)}, f32[1,128]{1,0:T(1,128)}) custom-call(f32[3,1,2,2,128]{4,3,2,1,0:T(2,128)} %frac_in.1, f32[1,2,2,128]{3,2,1,0:T(2,128)} %pol_in.1, s32[1,2,2,128]{3,2,1,0:T(2,128)} %occ_in.1, s32[1,2,2,27]{3,2,1,0:T(2,128)} %mask_in.1, f32[6,1,2,2,128]{4,3,2,1,0:T(2,128)} %perm_in.1, f32[6,6,1,2,2,128]{5,4,3,2,1,0:T(2,128)} %hist_in.1), custom_call_target="tpu_custom_call" | custom-call | tf_op jit(solution)/shard_map/pallas_call | solution.py:422
  57.2 0.0 copy-start
  57.2 1.3 %copy.10 = f32[6,1,2,2,128]{4,3,2,1,0:T(2,128)} copy(f32[6,1,2,2,128]{4,3,2,1,0:T(2,128)} %get-tuple-element.8) | data formatting | bytes 24576
  58.5 0.0 copy-done
Async XLA Ops:
  57.2 1.3 %copy-start = (f32[1,128]{1,0:T(1,128)S(1)}, f32[1,128]{1,0:T(1,128)}, u32[]{:S(2)}) copy-start(f32[1,128]{1,0:T(1,128)} %get-tuple-element.5) | copy-start | bytes 1540

commit v3 on v2

--- a/solution.py
+++ b/solution.py
@@ -89,7 +89,7 @@
     frac_in, pol_in, occ_in, mask_in, perm_in, hist_in,
     out_ref, change_ref,
     frac_ref, pol_ref, occ_ref, mask_ref, perm_ref, hist_ref,
-    geom, held_one, held_two, past_sets, own, radial, direct, sums, slots_a, slots_b,
+    geom, held_one, held_two, past_sets, own, apart, pull, direct, sums, slots_a, slots_b,
     load_sem, send_all, recv_all, send_geom, recv_geom, send_one, recv_one, send_two, recv_two,
 ):
     tiles = tuple(frac_ref.shape[1:4])
@@ -114,37 +114,46 @@
     for load in loads:
         load.start()
 
-    def coords(index):
-        return (index // (devices[1] * devices[2]), index // devices[2] % devices[1], index % devices[2])
+    def each_other(act):
+        def pair(step, carry):
+            ahead = (step // devices[1], step % devices[1])
+            first = []
+            for axis in range(2):
+                place = at[axis] + ahead[axis]
+                first.append(jnp.where(place >= devices[axis], place - devices[axis], place))
+            for shift in range(devices[2] - 1, -1, -1):
+                last = at[2] + shift
+                last = jnp.where(last >= devices[2], last - devices[2], last)
+                if shift == 0:
+                    @pl.when(step > 0)
+                    def _():
+                        act((first[0], first[1], last))
+                else:
+                    act((first[0], first[1], last))
+            return carry
+
+        lax.fori_loop(0, devices[0] * devices[1], pair, 0)
 
     barrier = pltpu.get_barrier_semaphore()
 
-    def greet(step, carry):
-        pl.semaphore_signal(
-            barrier, inc=1, device_id=coords((me + step) % total_devices), device_id_type=MESH
-        )
-        return carry
-
-    lax.fori_loop(1, total_devices, greet, 0)
+    each_other(
+        lambda device: pl.semaphore_signal(barrier, inc=1, device_id=device, device_id_type=MESH)
+    )
     for load in loads:
         load.wait()
 
     def everyone(index, held):
-        def one(step):
-            return pltpu.make_async_remote_copy(
+        def start(device):
+            pltpu.make_async_remote_copy(
                 src_ref=held.at[pl.ds(me, 1)],
                 dst_ref=held.at[pl.ds(me, 1)],
                 send_sem=send_all.at[index],
                 recv_sem=recv_all.at[index],
-                device_id=coords((me + step) % total_devices),
+                device_id=device,
                 device_id_type=MESH,
-            )
-
-        def start(step, carry):
-            one(step).start()
-            return carry
-
-        lax.fori_loop(1, total_devices, start, 0)
+            ).start()
+
+        each_other(start)
 
     def everyone_wait(index, held):
         whole = pltpu.make_async_remote_copy(
@@ -152,7 +161,7 @@
             dst_ref=held.at[pl.ds(0, total_devices - 1)],
             send_sem=send_all.at[index],
             recv_sem=recv_all.at[index],
-            device_id=coords((me + 1) % total_devices),
+            device_id=(at[0], at[1], (at[2] + 1) % devices[2]),
             device_id_type=MESH,
         )
         whole.wait_send()
@@ -228,8 +237,9 @@
         return carry
 
     lax.fori_loop(0, 2 * len(places), clear, 0)
-    for copy in geom_copies:
-        copy.wait()
+    for move, copy in zip(moves, geom_copies):
+        if move[0][0] == 0:
+            copy.wait()
 
     wraps = tuple(n + 2 for n in tiles)
 
@@ -245,8 +255,7 @@
     def source_rows(held, place, names):
         return [held[place[0], place[1], place[2], pl.ds(c, 1), :] for c in names]
 
-    def geometry(step, carry):
-        t, nine = step // 9, step % 9
+    def geometry(t, nine):
         along_x, along_y = nine // 3 - 1, nine % 3 - 1
         base = spot(t)
         for along_z in (-1, 0, 1):
@@ -273,12 +282,23 @@
                 three = 1.0 - fade
                 five = three - arg * fade
                 direct[t, k, part, :] = three * cube
-                radial[t, k, part, :] = five * cube * (3.0 * root_two)
+                radial = five * cube * (3.0 * root_two)
+                for i, d in enumerate((dx, dy, dz)):
+                    apart[i, t, k, part, :] = d
+                    pull[i, t, k, part, :] = radial * d
+
+    count = len(places)
+
+    def same_x(step, carry):
+        geometry(step // 3, 3 + step % 3)
         return carry
 
-    count = len(places)
-    early = count * 9 // 3
-    lax.fori_loop(0, early, geometry, 0)
+    def other_x(step, carry):
+        part = step % 6
+        geometry(step // 6, jnp.where(part < 3, part, part + 3))
+        return carry
+
+    lax.fori_loop(0, count * 3, same_x, 0)
 
     everyone_wait(0, slots_a)
     total = jnp.sum(slots_a[...], axis=0)
@@ -291,13 +311,15 @@
     one_copies = halo(held_one, send_one, recv_one)
     for copy in one_copies:
         copy.start()
-    lax.fori_loop(early, count * 9, geometry, 0)
+    for move, copy in zip(moves, geom_copies):
+        if move[0][0] != 0:
+            copy.wait()
+    lax.fori_loop(0, count * 6, other_x, 0)
     off_diagonal = lax.broadcasted_iota(jnp.int32, (slots, slots), 0) != lax.broadcasted_iota(
         jnp.int32, (slots, slots), 1
     )
     for t in range(count):
         direct[t, 13] = jnp.where(off_diagonal, direct[t, 13], 0.0)
-        radial[t, 13] = jnp.where(off_diagonal, radial[t, 13], 0.0)
 
     blocks = slots // FIELD_BLOCK
 
@@ -305,32 +327,27 @@
         part = pl.ds(pl.multiple_of(step % blocks * FIELD_BLOCK, FIELD_BLOCK), FIELD_BLOCK)
         t = (base[0] * tiles[1] + base[1]) * tiles[2] + base[2]
         place_y = wrap(base[1] + along_y, wraps[1])
-        target = [own[t, c, part, :] for c in range(3)]
-        target[1] = target[1] - CELL_EDGE * along_y.astype(jnp.float32)
-        deep = [target[2] - CELL_EDGE * along_z for along_z in (-1, 0, 1)]
 
         def plane(along_x, acc):
             acc = list(acc)
             place_x = wrap(base[0] + along_x, wraps[0])
-            wide = target[0] - CELL_EDGE * along_x
             for along_z in (-1, 0, 1):
                 place = (place_x, place_y, wrap(base[2] + along_z, wraps[2]))
-                source = source_rows(geom, place, range(3))
                 moment = source_rows(held, place, range(rows))
                 k = 9 * (along_x + 1) + 3 * (along_y + 1) + along_z + 1
-                r = radial[t, k, part, :]
                 d = direct[t, k, part, :]
-                apart = [source[0] - wide, source[1] - target[1], source[2] - deep[along_z + 1]]
+                away = [apart[i, t, k, part, :] for i in range(3)]
+                drawn = [pull[i, t, k, part, :] for i in range(3)]
                 for s in range(rows // 3):
                     m = moment[3 * s : 3 * s + 3]
-                    project = (apart[0] * m[0] + apart[1] * m[1] + apart[2] * m[2]) * r
+                    project = away[0] * m[0] + away[1] * m[1] + away[2] * m[2]
                     for i in range(3):
-                        acc[3 * s + i] = acc[3 * s + i] + (project * apart[i] - d * m[i])
+                        acc[3 * s + i] = acc[3 * s + i] + (project * drawn[i] - d * m[i])
             return tuple(acc)
 
-        acc = tuple(sums[index * count + t, c, part, :] for c in range(rows))
-        for along_x in (-1, 0, 1):
-            acc = plane(along_x, acc)
+        acc = lax.fori_loop(
+            -1, 2, plane, tuple(sums[index * count + t, c, part, :] for c in range(rows))
+        )
         for c in range(rows):
             sums[index * count + t, c, part, :] = acc[c]
 
@@ -439,7 +456,8 @@
                 pltpu.VMEM(wraps + (ROWS, slots), f32),
                 pltpu.VMEM((history.shape[0], count, ROWS, slots), f32),
                 pltpu.VMEM((count, 4, slots, slots), f32),
-                pltpu.VMEM((count, 27, slots, slots), f32),
+                pltpu.VMEM((3, count, 27, slots, slots), f32),
+                pltpu.VMEM((3, count, 27, slots, slots), f32),
                 pltpu.VMEM((count, 27, slots, slots), f32),
                 pltpu.VMEM((2 * count, rows, slots, slots), f32),
                 pltpu.VMEM((total_devices, 1, slots), f32),

time: 59.9 us -> 54.4 us (0.908)
  Pallas kernels: 56.6 us -> 51 us
    pallas_call x1, Pallas kernels: 56.6 us -> 51 us  [on_device(): pl.pallas_call(functools.partial(kernel, devices), out_shape=(jax.ShapeDt...]
where the time goes in v3:
time: 54.4 us; the launch traced here: 54.2 us
  Pallas kernels  51 us (94%)
  between operations  1.81 us (3%)
  local copies, waits for them, and re-layouts  1.31 us (2%)
    pallas_call x1, Pallas kernels, on_device(): pl.pallas_call(functools.partial(kernel, devices), out_shape=(jax.ShapeDt...  51 us
    unnamed x3, local copies, waits for them, and re-layouts  1.31 us

profile of v3, /device:TPU:0, one launch (start us, length us, event | category | flops | bytes accessed | tf_op | source)
XLA Modules:
  0.0 54.2 jit_solution(11962246032578375659)
XLA Ops:
  0.6 51.0 %shard_map.77 = (f32[6,1,2,2,128]{4,3,2,1,0:T(2,128)}, f32[1,128]{1,0:T(1,128)}) custom-call(f32[3,1,2,2,128]{4,3,2,1,0:T(2,128)} %frac_in.1, f32[1,2,2,128]{3,2,1,0:T(2,128)} %pol_in.1, s32[1,2,2,128]{3,2,1,0:T(2,128)} %occ_in.1, s32[1,2,2,27]{3,2,1,0:T(2,128)} %mask_in.1, f32[6,1,2,2,128]{4,3,2,1,0:T(2,128)} %perm_in.1, f32[6,6,1,2,2,128]{5,4,3,2,1,0:T(2,128)} %hist_in.1), custom_call_target="tpu_custom_call" | custom-call | tf_op jit(solution)/shard_map/pallas_call | solution.py:439
  51.7 0.0 copy-start
  51.7 1.3 %copy.10 = f32[6,1,2,2,128]{4,3,2,1,0:T(2,128)} copy(f32[6,1,2,2,128]{4,3,2,1,0:T(2,128)} %get-tuple-element.8) | data formatting | bytes 24576
  53.0 0.0 copy-done
Async XLA Ops:
  51.7 1.3 %copy-start = (f32[1,128]{1,0:T(1,128)S(1)}, f32[1,128]{1,0:T(1,128)}, u32[]{:S(2)}) copy-start(f32[1,128]{1,0:T(1,128)} %get-tuple-element.5) | copy-start | bytes 1540
